TPU v7x, 32 devices: a whole 2x2x4 slice. The times are simulated.
32 devices in a mesh: ctx: 8 (over z, x), heads: 4 (over y, core).
Axes of the slice: x: 2, y: 2, z: 4, core: 2. Of those that a mesh axis runs over, the one named last changes fastest.
Arguments:
- query_rows: bfloat16 [8, 16, 2, 128], P('ctx', 'heads'), may hold values from -6 to 6
- past_keys: bfloat16 [8, 16, 512, 128], P(None, 'heads', 'ctx'), may hold values from -6 to 6
- past_values: bfloat16 [8, 16, 512, 128], P(None, 'heads', 'ctx'), may hold values from -6 to 6
- used_length: int32 [8], replicated, may hold values from 256 to 512
Outputs:
- read: bfloat16 [8, 16, 2, 128], P('ctx', 'heads')
All inputs are finite; a program needn't handle non-finite values.
Results may differ from a plain program's by a relative error of at most 0.0015.
Values may be sent and summed in bfloat16 or wider, within the bound.
A program may use at most 64 MiB of HBM per device.

v0:
```python
import jax
import jax.numpy as jnp
from jax import lax
from jax.sharding import PartitionSpec as P

HEAD_SIZE = 128


def local(query_rows, past_keys, past_values, used_length):
    all_queries = lax.all_gather(query_rows, "ctx", axis=0, tiled=True)
    logit = jnp.einsum(
        "bkgd,bktd->bkgt", all_queries, past_keys, preferred_element_type=jnp.float32
    ) * HEAD_SIZE ** (-0.5)
    positions = lax.axis_index("ctx") * past_keys.shape[2] + jnp.arange(past_keys.shape[2])
    filled = positions[None, :] < used_length[:, None]
    logit = jnp.where(filled[:, None, None, :], logit, -1e30)
    top = jnp.max(logit, axis=-1)
    part = jnp.where(filled[:, None, None, :], jnp.exp(logit - top[..., None]), 0.0)
    weight_sum = jnp.sum(part, axis=-1)
    read_sum = jnp.einsum(
        "bkgt,bktd->bkgd", part, past_values.astype(jnp.float32), precision=lax.Precision.HIGHEST
    )
    tops, sums, parts = (
        lax.all_to_all(top[None], "ctx", split_axis=1, concat_axis=0, tiled=True),
        lax.all_to_all(weight_sum[None], "ctx", split_axis=1, concat_axis=0, tiled=True),
        lax.all_to_all(read_sum[None], "ctx", split_axis=1, concat_axis=0, tiled=True),
    )
    best = jnp.max(tops, axis=0)
    scale = jnp.exp(tops - best)
    weight_own = jnp.sum(sums * scale, axis=0)
    read_own = jnp.sum(parts * scale[..., None], axis=0)
    read = (read_own / weight_own[..., None]).astype(jnp.bfloat16)
    return read


def solution(mesh):
    return jax.shard_map(
        local,
        mesh=mesh,
        in_specs=(
            P("ctx", "heads", None, None),
            P(None, "heads", "ctx", None),
            P(None, "heads", "ctx", None),
            P(),
        ),
        out_specs=P("ctx", "heads", None, None),
        check_vma=False,
    )
```

profile of v0, /device:TPU:0, one launch (start us, length us, event | category | flops | bytes accessed | tf_op | source)
XLA Modules:
  0.0 62.1 jit_solution(10074065572557208397)
XLA Ops:
  0.0 0.0 copy-start
  0.0 0.0 copy-start.1
  0.0 0.7 %copy-done.1 = bf16[1,4,2,128]{3,2,1,0:T(2,128)(2,1)S(1)} copy-done((bf16[1,4,2,128]{3,2,1,0:T(2,128)(2,1)S(1)}, bf16[1,4,2,128]{3,2,1,0:T(2,128)(2,1)}, u32[]{:S(2)}) %copy-start.1) | copy-done | bytes 2072
  0.7 0.0 copy-start.2
  0.8 28.1 %all_gather.3 = bf16[8,4,2,128]{3,1,2,0:T(4,128)(2,1)S(1)} all-gather(bf16[1,4,2,128]{3,1,2,0:T(4,128)(2,1)S(1)} %copy.7), channel_id=1, replica_groups=mesh['ctx'=8,'heads'=4] {'ctx'}, dimensions={0}, use_global_device_ids=true | all-gather | bytes 18432 | tf_op jit(solution)/shard_map/all_gather | solution.py:10
  28.8 0.0 copy-done.2
  28.8 0.1 broadcast_compare_fusion
  28.9 1.5 %fusion.10 = (f32[8,4,2]{2,1,0:T(4,128)S(1)}, f32[8,4,2,64]{3,2,1,0:T(2,128)S(1)}) fusion(bf16[8,4,64,128]{3,2,1,0:T(8,128)(2,1)} %param.5, bf16[8,4,2,128]{3,1,2,0:T(4,128)(2,1)S(1)} %all_gather.3, pred[8,64]{1,0:T(8,128)(4,1)S(1)} %broadcast_compare_fusion), kind=kOutput, calls=%fused_computation.19 | convolution fusion | flops 1060800 | bytes 557824 | tf_op jit(solution)/shard_map/bkgd,bktd->bkgt/dot_general | solution.py:11
  30.4 0.7 %copy.11 = f32[1,8,4,2]{2,3,0,1:T(2,128)} copy(f32[1,8,4,2]{3,2,1,0:T(4,128)S(1)} %bitcast.30) | data formatting | bytes 512 | tf_op jit(solution)/shard_map/broadcast_in_dim | solution.py:24
  31.1 4.0 %all-to-all-start.1 = ((f32[1,8,4,2]{2,3,0,1:T(2,128)}), f32[1,8,4,2]{2,3,0,1:T(2,128)S(1)}, u32[]{:S(2)}, u32[]{:S(2)}) async-start(f32[1,8,4,2]{2,3,0,1:T(2,128)} %copy.11), calls=%async_computation.1 | async-start | bytes 16384 | tf_op jit(solution)/shard_map/all_to_all | solution.py:24
  35.1 0.0 copy-done
  35.1 1.2 %convolution_bitcast_fusion = f32[1,8,4,2,128]{4,3,2,0,1:T(2,128)} fusion(bf16[8,4,64,128]{3,2,1,0:T(8,128)(2,1)S(1)} %copy-done, f32[8,4,2,64]{3,2,1,0:T(2,128)S(1)} %get-tuple-element.6, pred[8,64]{1,0:T(8,128)(4,1)S(1)} %broadcast_compare_fusion, f32[8,4,2]{2,1,0:T(4,128)S(1)} %get-tuple-element.5), kind=kOutput, calls=%fused_computation | convolution fusion | flops 6299648 | bytes 574208 | tf_op jit(solution)/shard_map/bkgt,bktd->bkgd/dot_general | solution.py:20
  36.3 0.2 fusion.8
  36.5 0.7 %copy.15 = f32[1,8,4,2]{2,3,0,1:T(2,128)} copy(f32[1,8,4,2]{3,2,1,0:T(4,128)S(1)} %bitcast.31) | data formatting | bytes 512 | tf_op jit(solution)/shard_map/broadcast_in_dim | solution.py:25
  37.2 4.4 %all-to-all-done.1 = f32[1,8,4,2]{2,3,0,1:T(2,128)S(1)} async-done(((f32[1,8,4,2]{2,3,0,1:T(2,128)}), f32[1,8,4,2]{2,3,0,1:T(2,128)S(1)}, u32[]{:S(2)}, u32[]{:S(2)}) %all-to-all-start.1) | async-done | bytes 288 | tf_op jit(solution)/shard_map/all_to_all | solution.py:24
  41.6 3.3 %all-to-all-start.2 = ((f32[1,8,4,2]{2,3,0,1:T(2,128)}), f32[1,8,4,2]{2,3,0,1:T(2,128)S(1)}, u32[]{:S(2)}, u32[]{:S(2)}) async-start(f32[1,8,4,2]{2,3,0,1:T(2,128)} %copy.15), calls=%async_computation.2 | async-start | bytes 16384 | tf_op jit(solution)/shard_map/all_to_all | solution.py:25
  44.9 0.1 copy.12
  45.0 0.1 fusion.6
  45.1 6.3 %all-to-all-done.2 = f32[1,8,4,2]{2,3,0,1:T(2,128)S(1)} async-done(((f32[1,8,4,2]{2,3,0,1:T(2,128)}), f32[1,8,4,2]{2,3,0,1:T(2,128)S(1)}, u32[]{:S(2)}, u32[]{:S(2)}) %all-to-all-start.2) | async-done | bytes 288 | tf_op jit(solution)/shard_map/all_to_all | solution.py:25
  51.4 3.3 %all-to-all-start = ((f32[1,8,4,2,128]{4,3,2,0,1:T(2,128)}), f32[1,8,4,2,128]{4,3,2,0,1:T(2,128)S(1)}, u32[]{:S(2)}, u32[]{:S(2)}) async-start(f32[1,8,4,2,128]{4,3,2,0,1:T(2,128)} %convolution_bitcast_fusion), calls=%async_computation | async-start | bytes 65536 | tf_op jit(solution)/shard_map/all_to_all | solution.py:26
  54.7 0.1 copy.16
  54.8 0.2 fusion.5
  55.0 0.1 copy.18
  55.1 0.1 copy.13
  55.2 6.2 %all-to-all-done = f32[1,8,4,2,128]{4,3,2,0,1:T(2,128)S(1)} async-done(((f32[1,8,4,2,128]{4,3,2,0,1:T(2,128)}), f32[1,8,4,2,128]{4,3,2,0,1:T(2,128)S(1)}, u32[]{:S(2)}, u32[]{:S(2)}) %all-to-all-start) | async-done | bytes 32800 | tf_op jit(solution)/shard_map/all_to_all | solution.py:26
  61.4 0.1 fusion.1
  61.5 0.7 %fusion.7 = bf16[1,4,2,128]{3,2,1,0:T(2,128)(2,1)} fusion(f32[4,2,128]{2,1,0:T(2,128)S(1)} %fusion.1, f32[4,2]{1,0:T(4,128)S(1)} %copy.18), kind=kLoop, calls=%fused_computation.14 | loop fusion | flops 2048 | bytes 6176 | tf_op jit(solution)/shard_map/convert_element_type | solution.py:32
  (3 shorter events, 0.0 us)
Async XLA Ops:
  0.0 35.1 %copy-start = (bf16[8,4,64,128]{3,2,1,0:T(8,128)(2,1)S(1)}, bf16[8,4,64,128]{3,2,1,0:T(8,128)(2,1)}, u32[]{:S(2)}) copy-start(bf16[8,4,64,128]{3,2,1,0:T(8,128)(2,1)} %param.6) | copy-start | bytes 1572868
  0.0 0.7 %copy-start.1 = (bf16[1,4,2,128]{3,2,1,0:T(2,128)(2,1)S(1)}, bf16[1,4,2,128]{3,2,1,0:T(2,128)(2,1)}, u32[]{:S(2)}) copy-start(bf16[1,4,2,128]{3,2,1,0:T(2,128)(2,1)} %param.4) | copy-start | bytes 6148
  0.7 28.1 %copy-start.2 = (s32[8]{0:T(128)S(1)}, s32[8]{0:T(128)}, u32[]{:S(2)}) copy-start(s32[8]{0:T(128)} %param.7) | copy-start | bytes 100
  31.1 10.5 %all-to-all-start.1 = ((f32[1,8,4,2]{2,3,0,1:T(2,128)}), f32[1,8,4,2]{2,3,0,1:T(2,128)S(1)}, u32[]{:S(2)}, u32[]{:S(2)}) async-start(f32[1,8,4,2]{2,3,0,1:T(2,128)} %copy.11), calls=%async_computation.1 | async-start | bytes 16384 | tf_op jit(solution)/shard_map/all_to_all | solution.py:24
  41.6 9.8 %all-to-all-start.2 = ((f32[1,8,4,2]{2,3,0,1:T(2,128)}), f32[1,8,4,2]{2,3,0,1:T(2,128)S(1)}, u32[]{:S(2)}, u32[]{:S(2)}) async-start(f32[1,8,4,2]{2,3,0,1:T(2,128)} %copy.15), calls=%async_computation.2 | async-start | bytes 16384 | tf_op jit(solution)/shard_map/all_to_all | solution.py:25
  51.4 10.0 %all-to-all-start = ((f32[1,8,4,2,128]{4,3,2,0,1:T(2,128)}), f32[1,8,4,2,128]{4,3,2,0,1:T(2,128)S(1)}, u32[]{:S(2)}, u32[]{:S(2)}) async-start(f32[1,8,4,2,128]{4,3,2,0,1:T(2,128)} %convolution_bitcast_fusion), calls=%async_computation | async-start | bytes 65536 | tf_op jit(solution)/shard_map/all_to_all | solution.py:26
where the time goes:
time: 62.5 us; the launch traced here: 62.1 us
  blocking collectives  28.1 us (45%)
  waiting for transfers between devices  16.8 us (27%)
  starting transfers between devices  10.6 us (17%)
  matrix products  2.71 us (4%)
  local copies, waits for them, and re-layouts  2.59 us (4%)
  other arithmetic  1.32 us (2%)
    all_gather x1, blocking collectives, local(): all_queries = lax.all_gather(query_rows, 'ctx', axis=0, tiled=True)  28.1 us
    all_to_all x1, waiting for transfers between devices, local(): lax.all_to_all(weight_sum[None], 'ctx', split_axis=1, concat_axis=0, tile...  6.27 us
    all_to_all x1, waiting for transfers between devices, local(): lax.all_to_all(read_sum[None], 'ctx', split_axis=1, concat_axis=0, tiled=...  6.17 us
    all_to_all x1, waiting for transfers between devices, local(): lax.all_to_all(top[None], 'ctx', split_axis=1, concat_axis=0, tiled=True)  4.37 us
    all_to_all x1, starting transfers between devices, local(): lax.all_to_all(top[None], 'ctx', split_axis=1, concat_axis=0, tiled=True)  3.97 us
    all_to_all x1, starting transfers between devices, local(): lax.all_to_all(read_sum[None], 'ctx', split_axis=1, concat_axis=0, tiled=...  3.33 us
    all_to_all x1, starting transfers between devices, local(): lax.all_to_all(weight_sum[None], 'ctx', split_axis=1, concat_axis=0, tile...  3.32 us
    dot_general x1, matrix products, local(): jnp.einsum('bkgd,bktd->bkgt', all_queries, past_keys, preferred_element_t...  1.51 us
  transfers between devices with their start and end apart: 3, of which 3 were waited for; matrix products, arithmetic and copies ran while one was open for 4% of the time, Pallas kernels for 0%

commit v1 on v0

--- a/solution.py
+++ b/solution.py
@@ -6,8 +6,26 @@
 HEAD_SIZE = 128
 
 
+def gather_around(shard, axis, dim):
+    ways, here, step = (lax.axis_size(axis), lax.axis_index(axis), shard.shape[dim])
+    shape = [n * ways if d == dim else n for d, n in enumerate(shard.shape)]
+    full = lax.dynamic_update_slice_in_dim(
+        jnp.zeros(shape, shard.dtype), shard, here * step, axis=dim
+    )
+    going_up = going_down = shard
+    for far in range(1, ways // 2 + 1):
+        going_up = lax.ppermute(going_up, axis, [(d, (d + 1) % ways) for d in range(ways)])
+        full = lax.dynamic_update_slice_in_dim(full, going_up, (here - far) % ways * step, axis=dim)
+        if 2 * far < ways:
+            going_down = lax.ppermute(going_down, axis, [(d, (d - 1) % ways) for d in range(ways)])
+            full = lax.dynamic_update_slice_in_dim(
+                full, going_down, (here + far) % ways * step, axis=dim
+            )
+    return full
+
+
 def local(query_rows, past_keys, past_values, used_length):
-    all_queries = lax.all_gather(query_rows, "ctx", axis=0, tiled=True)
+    all_queries = gather_around(query_rows, "ctx", 0)
     logit = jnp.einsum(
         "bkgd,bktd->bkgt", all_queries, past_keys, preferred_element_type=jnp.float32
     ) * HEAD_SIZE ** (-0.5)

time: 62.5 us -> 59.5 us (0.952)
  blocking collectives: 28.1 us -> 0 us
  starting transfers between devices: 10.6 us -> 25.6 us
  waiting for transfers between devices: 16.8 us -> 26.2 us
  local copies, waits for them, and re-layouts: 2.59 us -> 3.29 us
    all_gather x1 -> x0, blocking collectives: 28.1 us -> none  [local(): all_queries = lax.all_gather(query_rows, 'ctx', axis=0, tiled=True)]
    ppermute x0 -> x7, starting transfers between devices: none -> 15.6 us  [the longest x3 12.6 us: gather_around(): lax.ppermute(going_down, axis, [(d, (d - 1) % ways) for d in range(ways)])]
    ppermute x0 -> x7, waiting for transfers between devices: none -> 9.48 us  [the longest x4 9.47 us: gather_around(): lax.ppermute(going_up, axis, [(d, (d + 1) % ways) for d in range(ways)])]
    all_to_all x1, starting transfers between devices: 3.97 us -> 3.29 us  [local(): lax.all_to_all(top[None], 'ctx', split_axis=1, concat_axis=0, tiled=True)]
    unnamed x7 -> x6, local copies, waits for them, and re-layouts: 0.75 us -> 1.35 us
  transfers between devices with their start and end apart: 3 -> 10, of which waited for: 3 -> 7; matrix products, arithmetic and copies ran while one was open for 4% -> 5% of each run, Pallas kernels for 0% -> 0%
where the time goes in v1:
time: 59.5 us; the launch traced here: 59.1 us
  waiting for transfers between devices  26.2 us (44%)
  starting transfers between devices  25.6 us (43%)
  local copies, waits for them, and re-layouts  3.29 us (6%)
  matrix products  2.71 us (5%)
  other arithmetic  1.32 us (2%)
    ppermute x3, starting transfers between devices, gather_around(): lax.ppermute(going_down, axis, [(d, (d - 1) % ways) for d in range(ways)])  12.6 us
    ppermute x4, waiting for transfers between devices, gather_around(): lax.ppermute(going_up, axis, [(d, (d + 1) % ways) for d in range(ways)])  9.47 us
    all_to_all x1, waiting for transfers between devices, local(): lax.all_to_all(weight_sum[None], 'ctx', split_axis=1, concat_axis=0, tile...  6.27 us
    all_to_all x1, waiting for transfers between devices, local(): lax.all_to_all(read_sum[None], 'ctx', split_axis=1, concat_axis=0, tiled=...  6.17 us
    all_to_all x1, waiting for transfers between devices, local(): lax.all_to_all(top[None], 'ctx', split_axis=1, concat_axis=0, tiled=True)  4.29 us
    all_to_all x1, starting transfers between devices, local(): lax.all_to_all(read_sum[None], 'ctx', split_axis=1, concat_axis=0, tiled=...  3.33 us
    all_to_all x1, starting transfers between devices, local(): lax.all_to_all(weight_sum[None], 'ctx', split_axis=1, concat_axis=0, tile...  3.32 us
    all_to_all x1, starting transfers between devices, local(): lax.all_to_all(top[None], 'ctx', split_axis=1, concat_axis=0, tiled=True)  3.29 us
  transfers between devices with their start and end apart: 10, of which 7 were waited for; matrix products, arithmetic and copies ran while one was open for 5% of the time, Pallas kernels for 0%

profile of v1, /device:TPU:0, one launch (start us, length us, event | category | flops | bytes accessed | tf_op | source)
XLA Modules:
  0.0 59.1 jit_solution(1120090613743013736)
XLA Ops:
  0.0 3.0 %collective-permute-start = (bf16[1,4,2,128]{3,2,1,0:T(2,128)(2,1)}, bf16[1,4,2,128]{3,2,1,0:T(2,128)(2,1)S(1)}, u32[]{:S(2)}, u32[]{:S(2)}) collective-permute-start(bf16[1,4,2,128]{3,2,1,0:T(2,128)(2,1)} %param.4), channel_id=1, source_target_pairs={{0,4},{4,8},{8,12},{12,16},{16,20},{20,24},{24,28},{28,0},{1,5},{5... | collective-permute-start | bytes 6152 | tf_op jit(solution)/shard_map/ppermute | solution.py:17
  3.0 3.1 %collective-permute-start.1 = (bf16[1,4,2,128]{3,2,1,0:T(2,128)(2,1)}, bf16[1,4,2,128]{3,2,1,0:T(2,128)(2,1)S(1)}, u32[]{:S(2)}, u32[]{:S(2)}) collective-permute-start(bf16[1,4,2,128]{3,2,1,0:T(2,128)(2,1)} %param.4), channel_id=1, source_target_pairs={{0,28},{4,0},{8,4},{12,8},{16,12},{20,16},{24,20},{28,24},{1,29},{... | collective-permute-start | bytes 6152 | tf_op jit(solution)/shard_map/ppermute | solution.py:20
  6.1 0.7 %copy-done.1 = bf16[1,4,2,128]{3,2,1,0:T(2,128)(2,1)S(1)} copy-done((bf16[1,4,2,128]{3,2,1,0:T(2,128)(2,1)S(1)}, bf16[1,4,2,128]{3,2,1,0:T(2,128)(2,1)}, u32[]{:S(2)}) %copy-start.1) | copy-done | bytes 2072
  6.8 0.6 %copy-done.2 = s32[8]{0:T(128)S(1)} copy-done((s32[8]{0:T(128)S(1)}, s32[8]{0:T(128)}, u32[]{:S(2)}) %copy-start.2) | copy-done | bytes 56
  7.4 0.1 broadcast_compare_fusion
  7.5 0.3 collective-permute-done
  7.8 4.8 %collective-permute-start.3 = (bf16[1,4,2,128]{3,2,1,0:T(2,128)(2,1)S(1)}, bf16[1,4,2,128]{3,2,1,0:T(2,128)(2,1)S(1)}, u32[]{:S(2)}, u32[]{:S(2)}) collective-permute-start(bf16[1,4,2,128]{3,2,1,0:T(2,128)(2,1)S(1)} %collective-permute-done.1), channel_id=1, source_target_pairs={{0,28},{4,0},{8,4},{12,8},{16,12},{20,16},{24,20},{28,24},{1,29},{... | collective-permute-start | bytes 6152 | tf_op jit(solution)/shard_map/ppermute | solution.py:20
  12.6 1.5 %collective-permute-done.2 = bf16[1,4,2,128]{3,2,1,0:T(2,128)(2,1)S(1)} collective-permute-done((bf16[1,4,2,128]{3,2,1,0:T(2,128)(2,1)S(1)}, bf16[1,4,2,128]{3,2,1,0:T(2,128)(2,1)S(1)}, u32[]{:S(2)}, u32[]{:S(2)}) %collective-permute-start.2) | collective-permute-done | bytes 2080 | tf_op jit(solution)/shard_map/ppermute | solution.py:17
  14.1 0.0 collective-permute-start.4
  14.1 0.0 collective-permute-done.3
  14.1 4.8 %collective-permute-start.5 = (bf16[1,4,2,128]{3,2,1,0:T(2,128)(2,1)S(1)}, bf16[1,4,2,128]{3,2,1,0:T(2,128)(2,1)S(1)}, u32[]{:S(2)}, u32[]{:S(2)}) collective-permute-start(bf16[1,4,2,128]{3,2,1,0:T(2,128)(2,1)S(1)} %collective-permute-done.3), channel_id=1, source_target_pairs={{0,28},{4,0},{8,4},{12,8},{16,12},{20,16},{24,20},{28,24},{1,29},{... | collective-permute-start | bytes 6152 | tf_op jit(solution)/shard_map/ppermute | solution.py:20
  18.9 1.5 %collective-permute-done.4 = bf16[1,4,2,128]{3,2,1,0:T(2,128)(2,1)S(1)} collective-permute-done((bf16[1,4,2,128]{3,2,1,0:T(2,128)(2,1)S(1)}, bf16[1,4,2,128]{3,2,1,0:T(2,128)(2,1)S(1)}, u32[]{:S(2)}, u32[]{:S(2)}) %collective-permute-start.4) | collective-permute-done | bytes 2080 | tf_op jit(solution)/shard_map/ppermute | solution.py:17
  20.4 6.2 %collective-permute-done.6 = bf16[1,4,2,128]{3,2,1,0:T(2,128)(2,1)S(1)} collective-permute-done((bf16[1,4,2,128]{3,2,1,0:T(2,128)(2,1)S(1)}, bf16[1,4,2,128]{3,2,1,0:T(2,128)(2,1)S(1)}, u32[]{:S(2)}, u32[]{:S(2)}) %collective-permute-start.6) | collective-permute-done | bytes 2080 | tf_op jit(solution)/shard_map/ppermute | solution.py:17
  26.6 1.5 %fusion.9 = (f32[8,4,2]{2,1,0:T(4,128)S(1)}, f32[8,4,2,64]{3,2,1,0:T(2,128)S(1)}) fusion(bf16[8,4,2,128]{3,2,1,0:T(2,128)(2,1)S(1)} %constant_dynamic-update-slice_fusion, bf16[8,4,64,128]{3,2,1,0:T(8,128)(2,1)} %param.5, pred[8,64]{1,0:T(8,128)(4,1)S(1)} %broadcast_compare_fusion), kind=kOutput, calls=%fused_computation.26 | convolution fusion | flops 1060800 | bytes 557824 | tf_op jit(solution)/shard_map/bkgd,bktd->bkgt/dot_general | solution.py:29
  28.1 0.7 %copy.9 = f32[1,8,4,2]{2,3,0,1:T(2,128)} copy(f32[1,8,4,2]{3,2,1,0:T(4,128)S(1)} %bitcast.31) | data formatting | bytes 512 | tf_op jit(solution)/shard_map/broadcast_in_dim | solution.py:42
  28.9 3.3 %all-to-all-start.1 = ((f32[1,8,4,2]{2,3,0,1:T(2,128)}), f32[1,8,4,2]{2,3,0,1:T(2,128)S(1)}, u32[]{:S(2)}, u32[]{:S(2)}) async-start(f32[1,8,4,2]{2,3,0,1:T(2,128)} %copy.9), calls=%async_computation.1 | async-start | bytes 16384 | tf_op jit(solution)/shard_map/all_to_all | solution.py:42
  32.2 1.2 %convolution_bitcast_fusion = f32[1,8,4,2,128]{4,3,2,0,1:T(2,128)} fusion(bf16[8,4,64,128]{3,2,1,0:T(8,128)(2,1)S(1)} %copy-done, f32[8,4,2,64]{3,2,1,0:T(2,128)S(1)} %get-tuple-element.6, pred[8,64]{1,0:T(8,128)(4,1)S(1)} %broadcast_compare_fusion, f32[8,4,2]{2,1,0:T(4,128)S(1)} %get-tuple-element.5), kind=kOutput, calls=%fused_computation | convolution fusion | flops 6299648 | bytes 574208 | tf_op jit(solution)/shard_map/bkgt,bktd->bkgd/dot_general | solution.py:38
  33.4 0.2 fusion.7
  33.6 0.7 %copy.13 = f32[1,8,4,2]{2,3,0,1:T(2,128)} copy(f32[1,8,4,2]{3,2,1,0:T(4,128)S(1)} %bitcast.32) | data formatting | bytes 512 | tf_op jit(solution)/shard_map/broadcast_in_dim | solution.py:43
  34.3 4.3 %all-to-all-done.1 = f32[1,8,4,2]{2,3,0,1:T(2,128)S(1)} async-done(((f32[1,8,4,2]{2,3,0,1:T(2,128)}), f32[1,8,4,2]{2,3,0,1:T(2,128)S(1)}, u32[]{:S(2)}, u32[]{:S(2)}) %all-to-all-start.1) | async-done | bytes 288 | tf_op jit(solution)/shard_map/all_to_all | solution.py:42
  38.6 3.3 %all-to-all-start.2 = ((f32[1,8,4,2]{2,3,0,1:T(2,128)}), f32[1,8,4,2]{2,3,0,1:T(2,128)S(1)}, u32[]{:S(2)}, u32[]{:S(2)}) async-start(f32[1,8,4,2]{2,3,0,1:T(2,128)} %copy.13), calls=%async_computation.2 | async-start | bytes 16384 | tf_op jit(solution)/shard_map/all_to_all | solution.py:43
  42.0 0.1 copy.10
  42.1 0.1 fusion.5
  42.1 6.3 %all-to-all-done.2 = f32[1,8,4,2]{2,3,0,1:T(2,128)S(1)} async-done(((f32[1,8,4,2]{2,3,0,1:T(2,128)}), f32[1,8,4,2]{2,3,0,1:T(2,128)S(1)}, u32[]{:S(2)}, u32[]{:S(2)}) %all-to-all-start.2) | async-done | bytes 288 | tf_op jit(solution)/shard_map/all_to_all | solution.py:43
  48.4 3.3 %all-to-all-start = ((f32[1,8,4,2,128]{4,3,2,0,1:T(2,128)}), f32[1,8,4,2,128]{4,3,2,0,1:T(2,128)S(1)}, u32[]{:S(2)}, u32[]{:S(2)}) async-start(f32[1,8,4,2,128]{4,3,2,0,1:T(2,128)} %convolution_bitcast_fusion), calls=%async_computation | async-start | bytes 65536 | tf_op jit(solution)/shard_map/all_to_all | solution.py:44
  51.8 0.1 copy.14
  51.8 0.2 fusion.4
  52.0 0.1 copy.16
  52.1 0.1 copy.11
  52.2 6.2 %all-to-all-done = f32[1,8,4,2,128]{4,3,2,0,1:T(2,128)S(1)} async-done(((f32[1,8,4,2,128]{4,3,2,0,1:T(2,128)}), f32[1,8,4,2,128]{4,3,2,0,1:T(2,128)S(1)}, u32[]{:S(2)}, u32[]{:S(2)}) %all-to-all-start) | async-done | bytes 32800 | tf_op jit(solution)/shard_map/all_to_all | solution.py:44
  58.4 0.1 fusion.1
  58.5 0.7 %fusion.6 = bf16[1,4,2,128]{3,2,1,0:T(2,128)(2,1)} fusion(f32[4,2,128]{2,1,0:T(2,128)S(1)} %fusion.1, f32[4,2]{1,0:T(4,128)S(1)} %copy.16), kind=kLoop, calls=%fused_computation.13 | loop fusion | flops 2048 | bytes 6176 | tf_op jit(solution)/shard_map/convert_element_type | solution.py:50
  (19 shorter events, 0.1 us)
Async XLA Ops:
  0.0 32.2 %copy-start = (bf16[8,4,64,128]{3,2,1,0:T(8,128)(2,1)S(1)}, bf16[8,4,64,128]{3,2,1,0:T(8,128)(2,1)}, u32[]{:S(2)}) copy-start(bf16[8,4,64,128]{3,2,1,0:T(8,128)(2,1)} %param.6) | copy-start | bytes 1572868
  0.0 7.8 %collective-permute-start = (bf16[1,4,2,128]{3,2,1,0:T(2,128)(2,1)}, bf16[1,4,2,128]{3,2,1,0:T(2,128)(2,1)S(1)}, u32[]{:S(2)}, u32[]{:S(2)}) collective-permute-start(bf16[1,4,2,128]{3,2,1,0:T(2,128)(2,1)} %param.4), channel_id=1, source_target_pairs={{0,4},{4,8},{8,12},{12,16},{16,20},{20,24},{24,28},{28,0},{1,5},{5... | collective-permute-start | bytes 6152 | tf_op jit(solution)/shard_map/ppermute | solution.py:17
  3.0 4.8 %collective-permute-start.1 = (bf16[1,4,2,128]{3,2,1,0:T(2,128)(2,1)}, bf16[1,4,2,128]{3,2,1,0:T(2,128)(2,1)S(1)}, u32[]{:S(2)}, u32[]{:S(2)}) collective-permute-start(bf16[1,4,2,128]{3,2,1,0:T(2,128)(2,1)} %param.4), channel_id=1, source_target_pairs={{0,28},{4,0},{8,4},{12,8},{16,12},{20,16},{24,20},{28,24},{1,29},{... | collective-permute-start | bytes 6152 | tf_op jit(solution)/shard_map/ppermute | solution.py:20
  6.1 0.7 %copy-start.1 = (bf16[1,4,2,128]{3,2,1,0:T(2,128)(2,1)S(1)}, bf16[1,4,2,128]{3,2,1,0:T(2,128)(2,1)}, u32[]{:S(2)}) copy-start(bf16[1,4,2,128]{3,2,1,0:T(2,128)(2,1)} %param.4) | copy-start | bytes 6148
  6.8 0.7 %copy-start.2 = (s32[8]{0:T(128)S(1)}, s32[8]{0:T(128)}, u32[]{:S(2)}) copy-start(s32[8]{0:T(128)} %param.7) | copy-start | bytes 100
  7.8 6.3 %collective-permute-start.2 = (bf16[1,4,2,128]{3,2,1,0:T(2,128)(2,1)S(1)}, bf16[1,4,2,128]{3,2,1,0:T(2,128)(2,1)S(1)}, u32[]{:S(2)}, u32[]{:S(2)}) collective-permute-start(bf16[1,4,2,128]{3,2,1,0:T(2,128)(2,1)S(1)} %collective-permute-done), channel_id=1, source_target_pairs={{0,4},{4,8},{8,12},{12,16},{16,20},{20,24},{24,28},{28,0},{1,5},{5... | collective-permute-start | bytes 6152 | tf_op jit(solution)/shard_map/ppermute | solution.py:17
  7.8 6.3 %collective-permute-start.3 = (bf16[1,4,2,128]{3,2,1,0:T(2,128)(2,1)S(1)}, bf16[1,4,2,128]{3,2,1,0:T(2,128)(2,1)S(1)}, u32[]{:S(2)}, u32[]{:S(2)}) collective-permute-start(bf16[1,4,2,128]{3,2,1,0:T(2,128)(2,1)S(1)} %collective-permute-done.1), channel_id=1, source_target_pairs={{0,28},{4,0},{8,4},{12,8},{16,12},{20,16},{24,20},{28,24},{1,29},{... | collective-permute-start | bytes 6152 | tf_op jit(solution)/shard_map/ppermute | solution.py:20
  14.1 6.3 %collective-permute-start.4 = (bf16[1,4,2,128]{3,2,1,0:T(2,128)(2,1)S(1)}, bf16[1,4,2,128]{3,2,1,0:T(2,128)(2,1)S(1)}, u32[]{:S(2)}, u32[]{:S(2)}) collective-permute-start(bf16[1,4,2,128]{3,2,1,0:T(2,128)(2,1)S(1)} %collective-permute-done.2), channel_id=1, source_target_pairs={{0,4},{4,8},{8,12},{12,16},{16,20},{20,24},{24,28},{28,0},{1,5},{5... | collective-permute-start | bytes 6152 | tf_op jit(solution)/shard_map/ppermute | solution.py:17
  14.1 6.3 %collective-permute-start.5 = (bf16[1,4,2,128]{3,2,1,0:T(2,128)(2,1)S(1)}, bf16[1,4,2,128]{3,2,1,0:T(2,128)(2,1)S(1)}, u32[]{:S(2)}, u32[]{:S(2)}) collective-permute-start(bf16[1,4,2,128]{3,2,1,0:T(2,128)(2,1)S(1)} %collective-permute-done.3), channel_id=1, source_target_pairs={{0,28},{4,0},{8,4},{12,8},{16,12},{20,16},{24,20},{28,24},{1,29},{... | collective-permute-start | bytes 6152 | tf_op jit(solution)/shard_map/ppermute | solution.py:20
  20.3 6.3 %collective-permute-start.6 = (bf16[1,4,2,128]{3,2,1,0:T(2,128)(2,1)S(1)}, bf16[1,4,2,128]{3,2,1,0:T(2,128)(2,1)S(1)}, u32[]{:S(2)}, u32[]{:S(2)}) collective-permute-start(bf16[1,4,2,128]{3,2,1,0:T(2,128)(2,1)S(1)} %collective-permute-done.4), channel_id=1, source_target_pairs={{0,4},{4,8},{8,12},{12,16},{16,20},{20,24},{24,28},{28,0},{1,5},{5... | collective-permute-start | bytes 6152 | tf_op jit(solution)/shard_map/ppermute | solution.py:17
  28.9 9.8 %all-to-all-start.1 = ((f32[1,8,4,2]{2,3,0,1:T(2,128)}), f32[1,8,4,2]{2,3,0,1:T(2,128)S(1)}, u32[]{:S(2)}, u32[]{:S(2)}) async-start(f32[1,8,4,2]{2,3,0,1:T(2,128)} %copy.9), calls=%async_computation.1 | async-start | bytes 16384 | tf_op jit(solution)/shard_map/all_to_all | solution.py:42
  38.6 9.8 %all-to-all-start.2 = ((f32[1,8,4,2]{2,3,0,1:T(2,128)}), f32[1,8,4,2]{2,3,0,1:T(2,128)S(1)}, u32[]{:S(2)}, u32[]{:S(2)}) async-start(f32[1,8,4,2]{2,3,0,1:T(2,128)} %copy.13), calls=%async_computation.2 | async-start | bytes 16384 | tf_op jit(solution)/shard_map/all_to_all | solution.py:43
  48.4 10.0 %all-to-all-start = ((f32[1,8,4,2,128]{4,3,2,0,1:T(2,128)}), f32[1,8,4,2,128]{4,3,2,0,1:T(2,128)S(1)}, u32[]{:S(2)}, u32[]{:S(2)}) async-start(f32[1,8,4,2,128]{4,3,2,0,1:T(2,128)} %convolution_bitcast_fusion), calls=%async_computation | async-start | bytes 65536 | tf_op jit(solution)/shard_map/all_to_all | solution.py:44
